TPU v7x, 256 devices: a 2x2x32 block of a 4x8x32 slice. The times are simulated.
256 devices in a mesh: groups: 4 (over x, y), seq: 64 (over z, core).
Axes of the slice: x: 2, y: 2, z: 32, core: 2. Of those that a mesh axis runs over, the one named last changes fastest.
The devices are a block of a 4x8x32 slice.
Arguments:
- queries: bfloat16 [32768, 4096], P(('groups', 'seq')), parts along dimension 0, may hold values from -100 to 100
- keys_values: bfloat16 [32768, 2, 512], P(('groups', 'seq')), parts along dimension 0, may hold values from -5 to 5
- head_signs: int32 [32, 128], replicated, may hold values from -1 to 1, as said below
- out_codes: int32 [512, 8192], P(None, 'seq'), may hold values from -2147483648 to 2147483647, as said below
- out_scales: bfloat16 [32, 8192], replicated, may hold values from 0.019897461 to 0.19921875
Outputs:
- projected: bfloat16 [32768, 8192], P(('groups', 'seq')), parts along dimension 0
There are 4 independent parts, one for each index of `groups`. A program takes and returns all parts, laid end to end along the dimension named above; an argument that names none is the same for every part. Nothing has to cross between parts.
Inputs may be any that keep to these rules, and one draw needn't show every extreme that they name: `head_signs`: every entry is -1 or 1. `out_codes`: each word holds eight codes of 0 to 15, the code of row 8 i + k in bits 4k to 4k + 3 of word row i, the word read as a signed 32-bit integer.
All inputs are finite; a program needn't handle non-finite values.
Results may differ from a plain program's by a relative error of at most 0.006.
Values may be sent and summed in bfloat16 or wider, within the bound.
A program may use at most 128 MiB of HBM per device.

v0:
```python
import math

import jax
import jax.numpy as jnp
from jax import lax
from jax.sharding import PartitionSpec as P

HEADS = 32
KV = 4
HD = 128
GROUP = 128
WINDOW = 2048


def passed_along(block, axis, distance):
    devices = range(lax.axis_size(axis))
    route = [(i - distance, i) for i in devices if i - distance in devices]
    return lax.ppermute(block, axis, route)


def hadamard(order):
    index = jnp.arange(order, dtype=jnp.int32)
    common = jnp.bitwise_and(index[:, None], index[None, :])
    ones = jnp.zeros((order, order), jnp.int32)
    for bit_index in range(order.bit_length()):
        ones = ones + jnp.bitwise_and(jnp.right_shift(common, bit_index), 1)
    return jnp.where(ones % 2 == 0, 1.0, -1.0).astype(jnp.float32)


def project(inputs, code_words, scale_cols):
    word_rows = code_words.shape[0]
    columns = code_words.shape[1]
    tok_rows = inputs.shape[0]
    group_words = GROUP // 8
    scale_rows = scale_cols.shape[0]
    tile_width = math.gcd(columns, 512)
    tile_count = columns // tile_width
    input_classes = jnp.transpose(inputs.reshape(tok_rows, word_rows, 8), (2, 0, 1))

    def one_tile(tile_index, output):
        begin = (tile_index * tile_width).astype(jnp.int32)
        tile_words = lax.dynamic_slice_in_dim(code_words, begin, tile_width, 1)
        tile_scales = lax.dynamic_slice_in_dim(scale_cols, begin, tile_width, 1).astype(jnp.float32)
        total = jnp.zeros((tok_rows, tile_width), jnp.float32)
        for nibble_index in range(8):
            code_vals = (
                jnp.bitwise_and(jnp.right_shift(tile_words, 4 * nibble_index), 15) - 8
            ).astype(jnp.float32)
            scaled = (
                code_vals.reshape(scale_rows, group_words, tile_width) * tile_scales[:, None, :]
            )
            weight = scaled.reshape(word_rows, tile_width).astype(jnp.bfloat16)
            total = total + jnp.dot(
                input_classes[nibble_index], weight, preferred_element_type=jnp.float32
            )
        return lax.dynamic_update_slice(output, total, (jnp.zeros((), jnp.int32), begin))

    initial = jnp.zeros((tok_rows, columns), jnp.float32)
    return lax.fori_loop(0, tile_count, one_tile, initial)


def on_device(queries, keys_values, head_signs, out_codes, out_scales):
    tok_rows = queries.shape[0]
    reach_blocks = (WINDOW + tok_rows - 2) // tok_rows
    my_start = lax.axis_index("seq") * tok_rows
    blocks = []
    current = keys_values
    for distance in range(reach_blocks):
        current = passed_along(current, "seq", 1)
        blocks.insert(0, current)
    window = jnp.concatenate(blocks + [keys_values], axis=0)
    key_count = window.shape[0]
    key_pos = my_start - reach_blocks * tok_rows + jnp.arange(key_count, dtype=jnp.int32)
    query_pos = my_start + jnp.arange(tok_rows, dtype=jnp.int32)
    distance_grid = query_pos[:, None] - key_pos[None, :]
    allowed = (distance_grid >= 0) & (distance_grid < WINDOW) & (key_pos[None, :] >= 0)
    allowed = allowed[None]
    per_group = HEADS // KV
    query_groups = jnp.transpose(queries.reshape(tok_rows, KV, per_group, HD), (1, 0, 2, 3))
    key_groups = jnp.transpose(window[:, 0].reshape(key_count, KV, HD), (1, 0, 2))
    value_groups = jnp.transpose(window[:, 1].reshape(key_count, KV, HD), (1, 0, 2))

    def attend(items):
        query_rows, key_rows, value_rows = items
        scores = jnp.einsum(
            "ihd,jd->hij", query_rows, key_rows, preferred_element_type=jnp.float32
        ) / math.sqrt(HD)
        scores = jnp.where(allowed, scores, -jnp.inf)
        row_max = jnp.max(scores, axis=-1, keepdims=True)
        weights = jnp.where(allowed, jnp.exp(scores - row_max), 0.0)
        total = jnp.sum(weights, axis=-1, keepdims=True)
        rounded = weights.astype(jnp.bfloat16)
        weighted = (
            jnp.einsum("hij,jd->hid", rounded, value_rows, preferred_element_type=jnp.float32)
            / total
        )
        return jnp.transpose(weighted, (1, 0, 2))

    attended = lax.map(attend, (query_groups, key_groups, value_groups))
    attended = jnp.transpose(attended, (1, 0, 2, 3)).reshape(tok_rows, HEADS, HD)
    signed = attended * head_signs.astype(jnp.float32)[None]
    mixed = jnp.einsum(
        "thd,de->the", signed, hadamard(HD), precision=lax.Precision.HIGHEST
    ) / math.sqrt(HD)
    rotated = mixed.astype(jnp.bfloat16).reshape(tok_rows, HEADS * HD)
    partial_out = project(rotated, lax.all_gather(out_codes, "seq", axis=1, tiled=True), out_scales)
    return partial_out.astype(jnp.bfloat16)


def solution(mesh):
    return jax.shard_map(
        on_device,
        mesh=mesh,
        in_specs=(
            P(("groups", "seq"), None),
            P(("groups", "seq"), None, None),
            P(),
            P(None, "seq"),
            P(),
        ),
        out_specs=P(("groups", "seq"), None),
        check_vma=False,
    )
```

profile of v0, /device:TPU:1316, one launch (start us, length us, event | category | flops | bytes accessed | tf_op | source)
XLA Modules:
  0.0 376.5 jit_solution(9635273169436782905)
XLA Ops:
  8.5 2.0 collective-permute-start
  10.4 7.0 %collective-permute-done = bf16[128,2,512]{0,2,1:T(8,128)(2,1)S(1)} collective-permute-done((bf16[128,2,512]{0,2,1:T(8,128)(2,1)S(1)}, bf16[128,2,512]{0,2,1:T(8,128)(2,1)S(1)}, u32[]{:S(2)}, u32[]{:S(2)}) %collective-permute-start) | collective-permute-done | bytes 262176 | tf_op jit(solution)/shard_map/ppermute | solution.py:18
  17.4 1.9 collective-permute-start.1
  19.3 7.0 %collective-permute-done.1 = bf16[128,2,512]{0,2,1:T(8,128)(2,1)S(1)} collective-permute-done((bf16[128,2,512]{0,2,1:T(8,128)(2,1)S(1)}, bf16[128,2,512]{0,2,1:T(8,128)(2,1)S(1)}, u32[]{:S(2)}, u32[]{:S(2)}) %collective-permute-start.1) | collective-permute-done | bytes 262176 | tf_op jit(solution)/shard_map/ppermute | solution.py:18
  26.3 1.9 collective-permute-start.2
  28.3 8.9 %collective-permute-done.2 = bf16[128,2,512]{0,2,1:T(8,128)(2,1)S(1)} collective-permute-done((bf16[128,2,512]{0,2,1:T(8,128)(2,1)S(1)}, bf16[128,2,512]{0,2,1:T(8,128)(2,1)S(1)}, u32[]{:S(2)}, u32[]{:S(2)}) %collective-permute-start.2) | collective-permute-done | bytes 262176 | tf_op jit(solution)/shard_map/ppermute | solution.py:18
  37.2 1.9 collective-permute-start.3
  39.1 9.2 %collective-permute-done.3 = bf16[128,2,512]{0,2,1:T(8,128)(2,1)S(1)} collective-permute-done((bf16[128,2,512]{0,2,1:T(8,128)(2,1)S(1)}, bf16[128,2,512]{0,2,1:T(8,128)(2,1)S(1)}, u32[]{:S(2)}, u32[]{:S(2)}) %collective-permute-start.3) | collective-permute-done | bytes 262176 | tf_op jit(solution)/shard_map/ppermute | solution.py:18
  48.3 1.9 collective-permute-start.4
  50.2 8.5 %collective-permute-done.4 = bf16[128,2,512]{0,2,1:T(8,128)(2,1)S(1)} collective-permute-done((bf16[128,2,512]{0,2,1:T(8,128)(2,1)S(1)}, bf16[128,2,512]{0,2,1:T(8,128)(2,1)S(1)}, u32[]{:S(2)}, u32[]{:S(2)}) %collective-permute-start.4) | collective-permute-done | bytes 262176 | tf_op jit(solution)/shard_map/ppermute | solution.py:18
  58.7 1.9 collective-permute-start.5
  60.6 12.2 %collective-permute-done.5 = bf16[128,2,512]{0,2,1:T(8,128)(2,1)S(1)} collective-permute-done((bf16[128,2,512]{0,2,1:T(8,128)(2,1)S(1)}, bf16[128,2,512]{0,2,1:T(8,128)(2,1)S(1)}, u32[]{:S(2)}, u32[]{:S(2)}) %collective-permute-start.5) | collective-permute-done | bytes 262176 | tf_op jit(solution)/shard_map/ppermute | solution.py:18
  72.8 1.9 collective-permute-start.6
  74.7 8.9 %collective-permute-done.6 = bf16[128,2,512]{0,2,1:T(8,128)(2,1)S(1)} collective-permute-done((bf16[128,2,512]{0,2,1:T(8,128)(2,1)S(1)}, bf16[128,2,512]{0,2,1:T(8,128)(2,1)S(1)}, u32[]{:S(2)}, u32[]{:S(2)}) %collective-permute-start.6) | collective-permute-done | bytes 262176 | tf_op jit(solution)/shard_map/ppermute | solution.py:18
  83.6 1.9 collective-permute-start.7
  85.6 9.7 %collective-permute-done.7 = bf16[128,2,512]{0,2,1:T(8,128)(2,1)S(1)} collective-permute-done((bf16[128,2,512]{0,2,1:T(8,128)(2,1)S(1)}, bf16[128,2,512]{0,2,1:T(8,128)(2,1)S(1)}, u32[]{:S(2)}, u32[]{:S(2)}) %collective-permute-start.7) | collective-permute-done | bytes 262176 | tf_op jit(solution)/shard_map/ppermute | solution.py:18
  95.3 1.9 collective-permute-start.8
  97.2 11.0 %collective-permute-done.8 = bf16[128,2,512]{0,2,1:T(8,128)(2,1)S(1)} collective-permute-done((bf16[128,2,512]{0,2,1:T(8,128)(2,1)S(1)}, bf16[128,2,512]{0,2,1:T(8,128)(2,1)S(1)}, u32[]{:S(2)}, u32[]{:S(2)}) %collective-permute-start.8) | collective-permute-done | bytes 262176 | tf_op jit(solution)/shard_map/ppermute | solution.py:18
  109.0 1.9 collective-permute-start.9
  110.9 9.6 %collective-permute-done.9 = bf16[128,2,512]{0,2,1:T(8,128)(2,1)S(1)} collective-permute-done((bf16[128,2,512]{0,2,1:T(8,128)(2,1)S(1)}, bf16[128,2,512]{0,2,1:T(8,128)(2,1)S(1)}, u32[]{:S(2)}, u32[]{:S(2)}) %collective-permute-start.9) | collective-permute-done | bytes 262176 | tf_op jit(solution)/shard_map/ppermute | solution.py:18
  121.2 1.9 collective-permute-start.10
  123.2 11.3 %collective-permute-done.10 = bf16[128,2,512]{0,2,1:T(8,128)(2,1)S(1)} collective-permute-done((bf16[128,2,512]{0,2,1:T(8,128)(2,1)S(1)}, bf16[128,2,512]{0,2,1:T(8,128)(2,1)S(1)}, u32[]{:S(2)}, u32[]{:S(2)}) %collective-permute-start.10) | collective-permute-done | bytes 262176 | tf_op jit(solution)/shard_map/ppermute | solution.py:18
  135.1 1.9 collective-permute-start.11
  137.1 8.2 %collective-permute-done.11 = bf16[128,2,512]{0,2,1:T(8,128)(2,1)S(1)} collective-permute-done((bf16[128,2,512]{0,2,1:T(8,128)(2,1)S(1)}, bf16[128,2,512]{0,2,1:T(8,128)(2,1)S(1)}, u32[]{:S(2)}, u32[]{:S(2)}) %collective-permute-start.11) | collective-permute-done | bytes 262176 | tf_op jit(solution)/shard_map/ppermute | solution.py:18
  146.0 1.9 collective-permute-start.12
  148.0 10.2 %collective-permute-done.12 = bf16[128,2,512]{0,2,1:T(8,128)(2,1)S(1)} collective-permute-done((bf16[128,2,512]{0,2,1:T(8,128)(2,1)S(1)}, bf16[128,2,512]{0,2,1:T(8,128)(2,1)S(1)}, u32[]{:S(2)}, u32[]{:S(2)}) %collective-permute-start.12) | collective-permute-done | bytes 262176 | tf_op jit(solution)/shard_map/ppermute | solution.py:18
  158.9 1.9 collective-permute-start.13
  160.8 7.8 %collective-permute-done.13 = bf16[128,2,512]{0,2,1:T(8,128)(2,1)S(1)} collective-permute-done((bf16[128,2,512]{0,2,1:T(8,128)(2,1)S(1)}, bf16[128,2,512]{0,2,1:T(8,128)(2,1)S(1)}, u32[]{:S(2)}, u32[]{:S(2)}) %collective-permute-start.13) | collective-permute-done | bytes 262176 | tf_op jit(solution)/shard_map/ppermute | solution.py:18
  168.7 1.9 collective-permute-start.14
  170.6 12.0 %collective-permute-done.14 = bf16[128,2,512]{0,2,1:T(8,128)(2,1)} collective-permute-done((bf16[128,2,512]{0,2,1:T(8,128)(2,1)S(1)}, bf16[128,2,512]{0,2,1:T(8,128)(2,1)}, u32[]{:S(2)}, u32[]{:S(2)}) %collective-permute-start.14) | collective-permute-done | bytes 262176 | tf_op jit(solution)/shard_map/ppermute | solution.py:18
  182.7 2.1 collective-permute-start.15
  189.5 3.1 collective-permute-done.15
  203.1 57.7 %while.28 = (s32[]{:T(128)}, f32[4,128,8,128]{3,1,2,0:T(8,128)}, bf16[4,2176,128]{1,2,0:T(8,128)(2,1)}, bf16[4,128,8,128]{1,3,2,0:T(8,128)(2,1)S(1)}, bf16[4,217...) while((s32[]{:T(128)}, f32[4,128,8,128]{3,1,2,0:T(8,128)}, ...), condition=%wide.region_3.4_spmd.clone, body=%wide.region_0.3_spmd.clone.sunk | while | flops 1155745920 | bytes 11670749 | solution.py:99
  203.1 2.4 fusion.169
  205.4 7.6 %fusion.170 = (f32[8,128]{1,0:T(8,128)}, bf16[8,128,2176]{1,2,0:T(8,128)(2,1)}) fusion(pred[128,2176]{0,1:T(8,128)(4,1)S(1)} %fusion.169, bf16[4,2176,128]{1,2,0:T(8,128)(2,1)} %get-tuple-element.382, s32[]{:T(128)} %get-tuple-element.371, bf16[4,128,8,128]{1,3,2,0:T(8,128)(2,1)S(1)} %get-tuple-element.383), kind=kOutput, calls=%fused_computation.131.clone.1 | convolution fusion | flops 583796864 | bytes 5837824 | tf_op jit(solution)/shard_map/while/body/eval_jaxpr/sub | solution.py:90
  213.1 4.4 %fusion.171 = f32[4,128,8,128]{3,1,2,0:T(8,128)} fusion(f32[4,128,8,128]{3,1,2,0:T(8,128)} %get-tuple-element.372, s32[]{:T(128)} %get-tuple-element.371, bf16[8,128,2176]{1,2,0:T(8,128)(2,1)} %get-tuple-element.360, bf16[4,2176,128]{1,2,0:T(8,128)(2,1)S(1)} %get-tuple-element.384, f32[128,8]{0,1:T(8,128)} %bitcast.188), kind=kOutput, calls=%fused_computation.59.clone.1 | convolution fusion | flops 570556416 | bytes 5542912 | tf_op jit(solution)/shard_map/while/body/eval_jaxpr/hij,jd->hid/dot_general | solution.py:94
  217.5 2.4 fusion.169
  219.9 7.6 %fusion.170 = (f32[8,128]{1,0:T(8,128)}, bf16[8,128,2176]{1,2,0:T(8,128)(2,1)}) fusion(pred[128,2176]{0,1:T(8,128)(4,1)S(1)} %fusion.169, bf16[4,2176,128]{1,2,0:T(8,128)(2,1)} %get-tuple-element.382, s32[]{:T(128)} %get-tuple-element.371, bf16[4,128,8,128]{1,3,2,0:T(8,128)(2,1)S(1)} %get-tuple-element.383), kind=kOutput, calls=%fused_computation.131.clone.1 | convolution fusion | flops 583796864 | bytes 5837824 | tf_op jit(solution)/shard_map/while/body/eval_jaxpr/sub | solution.py:90
  227.5 4.4 %fusion.171 = f32[4,128,8,128]{3,1,2,0:T(8,128)} fusion(f32[4,128,8,128]{3,1,2,0:T(8,128)} %get-tuple-element.372, s32[]{:T(128)} %get-tuple-element.371, bf16[8,128,2176]{1,2,0:T(8,128)(2,1)} %get-tuple-element.360, bf16[4,2176,128]{1,2,0:T(8,128)(2,1)S(1)} %get-tuple-element.384, f32[128,8]{0,1:T(8,128)} %bitcast.188), kind=kOutput, calls=%fused_computation.59.clone.1 | convolution fusion | flops 570556416 | bytes 5542912 | tf_op jit(solution)/shard_map/while/body/eval_jaxpr/hij,jd->hid/dot_general | solution.py:94
  231.9 2.4 fusion.169
  234.3 7.6 %fusion.170 = (f32[8,128]{1,0:T(8,128)}, bf16[8,128,2176]{1,2,0:T(8,128)(2,1)}) fusion(pred[128,2176]{0,1:T(8,128)(4,1)S(1)} %fusion.169, bf16[4,2176,128]{1,2,0:T(8,128)(2,1)} %get-tuple-element.382, s32[]{:T(128)} %get-tuple-element.371, bf16[4,128,8,128]{1,3,2,0:T(8,128)(2,1)S(1)} %get-tuple-element.383), kind=kOutput, calls=%fused_computation.131.clone.1 | convolution fusion | flops 583796864 | bytes 5837824 | tf_op jit(solution)/shard_map/while/body/eval_jaxpr/sub | solution.py:90
  241.9 4.4 %fusion.171 = f32[4,128,8,128]{3,1,2,0:T(8,128)} fusion(f32[4,128,8,128]{3,1,2,0:T(8,128)} %get-tuple-element.372, s32[]{:T(128)} %get-tuple-element.371, bf16[8,128,2176]{1,2,0:T(8,128)(2,1)} %get-tuple-element.360, bf16[4,2176,128]{1,2,0:T(8,128)(2,1)S(1)} %get-tuple-element.384, f32[128,8]{0,1:T(8,128)} %bitcast.188), kind=kOutput, calls=%fused_computation.59.clone.1 | convolution fusion | flops 570556416 | bytes 5542912 | tf_op jit(solution)/shard_map/while/body/eval_jaxpr/hij,jd->hid/dot_general | solution.py:94
  246.4 2.4 fusion.169
  248.7 7.6 %fusion.170 = (f32[8,128]{1,0:T(8,128)}, bf16[8,128,2176]{1,2,0:T(8,128)(2,1)}) fusion(pred[128,2176]{0,1:T(8,128)(4,1)S(1)} %fusion.169, bf16[4,2176,128]{1,2,0:T(8,128)(2,1)} %get-tuple-element.382, s32[]{:T(128)} %get-tuple-element.371, bf16[4,128,8,128]{1,3,2,0:T(8,128)(2,1)S(1)} %get-tuple-element.383), kind=kOutput, calls=%fused_computation.131.clone.1 | convolution fusion | flops 583796864 | bytes 5837824 | tf_op jit(solution)/shard_map/while/body/eval_jaxpr/sub | solution.py:90
  256.4 4.4 %fusion.171 = f32[4,128,8,128]{3,1,2,0:T(8,128)} fusion(f32[4,128,8,128]{3,1,2,0:T(8,128)} %get-tuple-element.372, s32[]{:T(128)} %get-tuple-element.371, bf16[8,128,2176]{1,2,0:T(8,128)(2,1)} %get-tuple-element.360, bf16[4,2176,128]{1,2,0:T(8,128)(2,1)S(1)} %get-tuple-element.384, f32[128,8]{0,1:T(8,128)} %bitcast.188), kind=kOutput, calls=%fused_computation.59.clone.1 | convolution fusion | flops 570556416 | bytes 5542912 | tf_op jit(solution)/shard_map/while/body/eval_jaxpr/hij,jd->hid/dot_general | solution.py:94
  262.6 2.1 multiply_convert_fusion
  265.7 101.0 %while.27 = (s32[]{:T(128)}, bf16[128,8192]{0,1:T(8,128)(2,1)S(1)}, s32[512,8192]{1,0:T(8,128)}, bf16[32,8192]{1,0:T(8,128)(2,1)}, bf16[8,128,512]{2,1,0:T(8,128...) while((s32[]{:T(128)}, bf16[128,8192]{0,1:T(8,128)(2,1)S(1)}, s32[512,8192]{1,0:T(8,128)}, ...), condition=%wide.region_5.6_spmd, body=%wide.region_4.5_spmd.sunk | while | flops 549928960 | bytes 14581911 | solution.py:59
  266.7 2.7 fusion.162
  273.0 2.7 fusion.162
  279.3 2.7 fusion.162
  285.6 2.7 fusion.162
  291.9 2.7 fusion.162
  298.2 2.7 fusion.162
  304.5 2.7 fusion.162
  310.8 2.7 fusion.162
  317.1 2.7 fusion.162
  323.4 2.7 fusion.162
  329.7 2.7 fusion.162
  336.0 2.7 fusion.162
  342.3 2.7 fusion.162
  348.6 2.7 fusion.162
  354.9 2.7 fusion.162
  361.2 2.7 fusion.162
  366.7 2.9 copy.17
  (187 shorter events, 80.0 us)
Async XLA Ops:
  6.5 258.9 %all-gather.2.cloned.1.call-start = ((), (), s32[]{:S(2)}) async-start(), calls=%async_computation | async-start | bytes 17039360 | tf_op jit(solution)/shard_map/all_gather | solution.py:106
  8.5 8.9 %collective-permute-start = (bf16[128,2,512]{0,2,1:T(8,128)(2,1)S(1)}, bf16[128,2,512]{0,2,1:T(8,128)(2,1)S(1)}, u32[]{:S(2)}, u32[]{:S(2)}) collective-permute-start(bf16[128,2,512]{0,2,1:T(8,128)(2,1)S(1)} %copy.10), channel_id=1, source_target_pairs={{0,1},{1,2},{2,3},{3,4},{4,5},{5,6},{6,7},{7,8},{8,9},{9,10},{10,1... | collective-permute-start | bytes 786440 | tf_op jit(solution)/shard_map/ppermute | solution.py:18
  17.4 8.9 %collective-permute-start.1 = (bf16[128,2,512]{0,2,1:T(8,128)(2,1)S(1)}, bf16[128,2,512]{0,2,1:T(8,128)(2,1)S(1)}, u32[]{:S(2)}, u32[]{:S(2)}) collective-permute-start(bf16[128,2,512]{0,2,1:T(8,128)(2,1)S(1)} %collective-permute-done), channel_id=1, source_target_pairs={{0,1},{1,2},{2,3},{3,4},{4,5},{5,6},{6,7},{7,8},{8,9},{9,10},{10,1... | collective-permute-start | bytes 786440 | tf_op jit(solution)/shard_map/ppermute | solution.py:18
  26.3 10.9 %collective-permute-start.2 = (bf16[128,2,512]{0,2,1:T(8,128)(2,1)S(1)}, bf16[128,2,512]{0,2,1:T(8,128)(2,1)S(1)}, u32[]{:S(2)}, u32[]{:S(2)}) collective-permute-start(bf16[128,2,512]{0,2,1:T(8,128)(2,1)S(1)} %collective-permute-done.1), channel_id=1, source_target_pairs={{0,1},{1,2},{2,3},{3,4},{4,5},{5,6},{6,7},{7,8},{8,9},{9,10},{10,1... | collective-permute-start | bytes 786440 | tf_op jit(solution)/shard_map/ppermute | solution.py:18
  37.2 11.1 %collective-permute-start.3 = (bf16[128,2,512]{0,2,1:T(8,128)(2,1)S(1)}, bf16[128,2,512]{0,2,1:T(8,128)(2,1)S(1)}, u32[]{:S(2)}, u32[]{:S(2)}) collective-permute-start(bf16[128,2,512]{0,2,1:T(8,128)(2,1)S(1)} %collective-permute-done.2), channel_id=1, source_target_pairs={{0,1},{1,2},{2,3},{3,4},{4,5},{5,6},{6,7},{7,8},{8,9},{9,10},{10,1... | collective-permute-start | bytes 786440 | tf_op jit(solution)/shard_map/ppermute | solution.py:18
  48.3 10.4 %collective-permute-start.4 = (bf16[128,2,512]{0,2,1:T(8,128)(2,1)S(1)}, bf16[128,2,512]{0,2,1:T(8,128)(2,1)S(1)}, u32[]{:S(2)}, u32[]{:S(2)}) collective-permute-start(bf16[128,2,512]{0,2,1:T(8,128)(2,1)S(1)} %collective-permute-done.3), channel_id=1, source_target_pairs={{0,1},{1,2},{2,3},{3,4},{4,5},{5,6},{6,7},{7,8},{8,9},{9,10},{10,1... | collective-permute-start | bytes 786440 | tf_op jit(solution)/shard_map/ppermute | solution.py:18
  58.7 14.1 %collective-permute-start.5 = (bf16[128,2,512]{0,2,1:T(8,128)(2,1)S(1)}, bf16[128,2,512]{0,2,1:T(8,128)(2,1)S(1)}, u32[]{:S(2)}, u32[]{:S(2)}) collective-permute-start(bf16[128,2,512]{0,2,1:T(8,128)(2,1)S(1)} %collective-permute-done.4), channel_id=1, source_target_pairs={{0,1},{1,2},{2,3},{3,4},{4,5},{5,6},{6,7},{7,8},{8,9},{9,10},{10,1... | collective-permute-start | bytes 786440 | tf_op jit(solution)/shard_map/ppermute | solution.py:18
  72.8 10.8 %collective-permute-start.6 = (bf16[128,2,512]{0,2,1:T(8,128)(2,1)S(1)}, bf16[128,2,512]{0,2,1:T(8,128)(2,1)S(1)}, u32[]{:S(2)}, u32[]{:S(2)}) collective-permute-start(bf16[128,2,512]{0,2,1:T(8,128)(2,1)S(1)} %collective-permute-done.5), channel_id=1, source_target_pairs={{0,1},{1,2},{2,3},{3,4},{4,5},{5,6},{6,7},{7,8},{8,9},{9,10},{10,1... | collective-permute-start | bytes 786440 | tf_op jit(solution)/shard_map/ppermute | solution.py:18
  83.6 11.7 %collective-permute-start.7 = (bf16[128,2,512]{0,2,1:T(8,128)(2,1)S(1)}, bf16[128,2,512]{0,2,1:T(8,128)(2,1)S(1)}, u32[]{:S(2)}, u32[]{:S(2)}) collective-permute-start(bf16[128,2,512]{0,2,1:T(8,128)(2,1)S(1)} %collective-permute-done.6), channel_id=1, source_target_pairs={{0,1},{1,2},{2,3},{3,4},{4,5},{5,6},{6,7},{7,8},{8,9},{9,10},{10,1... | collective-permute-start | bytes 786440 | tf_op jit(solution)/shard_map/ppermute | solution.py:18
  95.3 13.0 %collective-permute-start.8 = (bf16[128,2,512]{0,2,1:T(8,128)(2,1)S(1)}, bf16[128,2,512]{0,2,1:T(8,128)(2,1)S(1)}, u32[]{:S(2)}, u32[]{:S(2)}) collective-permute-start(bf16[128,2,512]{0,2,1:T(8,128)(2,1)S(1)} %collective-permute-done.7), channel_id=1, source_target_pairs={{0,1},{1,2},{2,3},{3,4},{4,5},{5,6},{6,7},{7,8},{8,9},{9,10},{10,1... | collective-permute-start | bytes 786440 | tf_op jit(solution)/shard_map/ppermute | solution.py:18
  108.3 0.7 copy-start
  109.0 11.5 %collective-permute-start.9 = (bf16[128,2,512]{0,2,1:T(8,128)(2,1)S(1)}, bf16[128,2,512]{0,2,1:T(8,128)(2,1)S(1)}, u32[]{:S(2)}, u32[]{:S(2)}) collective-permute-start(bf16[128,2,512]{0,2,1:T(8,128)(2,1)S(1)} %collective-permute-done.8), channel_id=1, source_target_pairs={{0,1},{1,2},{2,3},{3,4},{4,5},{5,6},{6,7},{7,8},{8,9},{9,10},{10,1... | collective-permute-start | bytes 786440 | tf_op jit(solution)/shard_map/ppermute | solution.py:18
  120.5 0.7 copy-start.1
  121.2 13.2 %collective-permute-start.10 = (bf16[128,2,512]{0,2,1:T(8,128)(2,1)S(1)}, bf16[128,2,512]{0,2,1:T(8,128)(2,1)S(1)}, u32[]{:S(2)}, u32[]{:S(2)}) collective-permute-start(bf16[128,2,512]{0,2,1:T(8,128)(2,1)S(1)} %collective-permute-done.9), channel_id=1, source_target_pairs={{0,1},{1,2},{2,3},{3,4},{4,5},{5,6},{6,7},{7,8},{8,9},{9,10},{10,1... | collective-permute-start | bytes 786440 | tf_op jit(solution)/shard_map/ppermute | solution.py:18
  134.4 0.7 copy-start.2
  135.1 10.2 %collective-permute-start.11 = (bf16[128,2,512]{0,2,1:T(8,128)(2,1)S(1)}, bf16[128,2,512]{0,2,1:T(8,128)(2,1)S(1)}, u32[]{:S(2)}, u32[]{:S(2)}) collective-permute-start(bf16[128,2,512]{0,2,1:T(8,128)(2,1)S(1)} %collective-permute-done.10), channel_id=1, source_target_pairs={{0,1},{1,2},{2,3},{3,4},{4,5},{5,6},{6,7},{7,8},{8,9},{9,10},{10,1... | collective-permute-start | bytes 786440 | tf_op jit(solution)/shard_map/ppermute | solution.py:18
  145.3 0.7 copy-start.3
  146.0 12.2 %collective-permute-start.12 = (bf16[128,2,512]{0,2,1:T(8,128)(2,1)S(1)}, bf16[128,2,512]{0,2,1:T(8,128)(2,1)S(1)}, u32[]{:S(2)}, u32[]{:S(2)}) collective-permute-start(bf16[128,2,512]{0,2,1:T(8,128)(2,1)S(1)} %collective-permute-done.11), channel_id=1, source_target_pairs={{0,1},{1,2},{2,3},{3,4},{4,5},{5,6},{6,7},{7,8},{8,9},{9,10},{10,1... | collective-permute-start | bytes 786440 | tf_op jit(solution)/shard_map/ppermute | solution.py:18
  158.2 0.7 copy-start.4
  158.9 9.8 %collective-permute-start.13 = (bf16[128,2,512]{0,2,1:T(8,128)(2,1)S(1)}, bf16[128,2,512]{0,2,1:T(8,128)(2,1)S(1)}, u32[]{:S(2)}, u32[]{:S(2)}) collective-permute-start(bf16[128,2,512]{0,2,1:T(8,128)(2,1)S(1)} %collective-permute-done.12), channel_id=1, source_target_pairs={{0,1},{1,2},{2,3},{3,4},{4,5},{5,6},{6,7},{7,8},{8,9},{9,10},{10,1... | collective-permute-start | bytes 786440 | tf_op jit(solution)/shard_map/ppermute | solution.py:18
  168.7 16.7 %copy-start.5 = (bf16[128,2,512]{0,2,1:T(8,128)(2,1)}, bf16[128,2,512]{0,2,1:T(8,128)(2,1)S(1)}, u32[]{:S(2)}) copy-start(bf16[128,2,512]{0,2,1:T(8,128)(2,1)S(1)} %collective-permute-done.13) | copy-start | bytes 786436
  168.7 14.0 %collective-permute-start.14 = (bf16[128,2,512]{0,2,1:T(8,128)(2,1)S(1)}, bf16[128,2,512]{0,2,1:T(8,128)(2,1)}, u32[]{:S(2)}, u32[]{:S(2)}) collective-permute-start(bf16[128,2,512]{0,2,1:T(8,128)(2,1)S(1)} %collective-permute-done.13), channel_id=1, source_target_pairs={{0,1},{1,2},{2,3},{3,4},{4,5},{5,6},{6,7},{7,8},{8,9},{9,10},{10,1... | collective-permute-start | bytes 786440 | tf_op jit(solution)/shard_map/ppermute | solution.py:18
  182.7 9.9 %collective-permute-start.15 = (bf16[128,2,512]{0,2,1:T(8,128)(2,1)}, bf16[128,2,512]{0,2,1:T(8,128)(2,1)}, u32[]{:S(2)}, u32[]{:S(2)}) collective-permute-start(bf16[128,2,512]{0,2,1:T(8,128)(2,1)} %collective-permute-done.14), channel_id=1, source_target_pairs={{0,1},{1,2},{2,3},{3,4},{4,5},{5,6},{6,7},{7,8},{8,9},{9,10},{10,1... | collective-permute-start | bytes 786440 | tf_op jit(solution)/shard_map/ppermute | solution.py:18
Sparse Core Ops, SparseCore 0:
  9.1 194.5 all-gather.1
where the time goes:
time: 380 us; the launch traced here: 376 us
  waiting for transfers between devices  145 us (38%)
  matrix products  94.7 us (25%)
  other arithmetic  69.7 us (18%)
  starting transfers between devices  31.2 us (8%)
  local copies, waits for them, and re-layouts  20.6 us (5%)
  between operations  13.7 us (4%)
    ppermute x16, waiting for transfers between devices, passed_along(): return lax.ppermute(block, axis, route)  144 us
    dot_general x128, matrix products, one_tile(): jnp.dot(input_classes[nibble_index], weight, preferred_element_type=jnp.f...  44.4 us
    convert_element_type x16, other arithmetic, one_tile(): weight = scaled.reshape(word_rows, tile_width).astype(jnp.bfloat16)  43.1 us
    ppermute x16, starting transfers between devices, passed_along(): return lax.ppermute(block, axis, route)  31.2 us
    sub x4, matrix products, attend(): weights = jnp.where(allowed, jnp.exp(scores - row_max), 0.0)  30.5 us
    dot_general x4, matrix products, attend(): jnp.einsum('hij,jd->hid', rounded, value_rows, preferred_element_type=jnp...  17.8 us
    unnamed x30, local copies, waits for them, and re-layouts  14.9 us
    convert_element_type x16, other arithmetic, one_tile(): lax.dynamic_slice_in_dim(scale_cols, begin, tile_width, 1)  12.3 us
  transfers between devices with their start and end apart: 17, of which 16 were waited for; matrix products, arithmetic and copies ran while one was open for 21% of the time, Pallas kernels for 0%

commit v1 on v0

v1 whole, which is shorter than its diff:
```python
import functools
import math

import jax
import jax.numpy as jnp
import numpy as np
from jax import lax
from jax.experimental import pallas as pl
from jax.experimental.pallas import tpu as pltpu
from jax.sharding import PartitionSpec as P

HEADS = 32
KV = 4
HD = 128
WINDOW = 2048
CORES = 2
MESH = pl.DeviceIdType.MESH
F32 = jnp.float32
BF16 = jnp.bfloat16


def hadamard_columns():
    d = np.arange(HD)
    e = np.array([8 * i + k for k in range(8) for i in range(HD // 8)])
    common = d[:, None] & e[None, :]
    bits = sum((common >> b) & 1 for b in range(HD.bit_length()))
    return np.where(bits % 2 == 0, 1.0, -1.0).astype(np.float32)


def kernel(
    plane_y,
    queries, kvt, codes_in, scales, signs, had,
    out,
    codes, kv, q, acc, top, xr, wbuf, obuf, sc,
    zm_recv, zp_recv, kv_recv, xy_recv,
    zm_send, zp_send, kv_send, xy_send,
    load_sem, pair_send, pair_recv, xr_send, xr_recv, out_local, out_send, out_recv,
):
    ns = lax.axis_size("seq")
    nz = ns // CORES
    g = lax.axis_index("groups")
    s = lax.axis_index("seq")
    z = s // CORES
    c = s % CORES
    tok = queries.shape[0]
    rows = tok * CORES
    half_heads = HEADS // CORES
    width = half_heads * HD
    hops = WINDOW // rows
    words = codes_in.shape[0]
    half, quarter = words // 2, words // 4

    gx_, gy_ = g // plane_y, g % plane_y
    across_x = (gx_ + 1 - 2 * (gx_ % 2)) * plane_y + gy_
    across_y = gx_ * plane_y + gy_ + 1 - 2 * (gy_ % 2)
    parity = (gx_ + gy_) % 2
    partner = (g, z * CORES + 1 - c)
    up = (g, (s + CORES) % ns)
    down = (g, (s + ns - CORES) % ns)

    down_steps_a = 3 * hops // 2
    up_steps = (nz - 1 - down_steps_a) // 2 + 1
    down_steps = nz - 1 - up_steps

    barrier = pltpu.get_barrier_semaphore()
    for dev in (partner, up, down, (across_x, s), (across_y, s)):
        pl.semaphore_signal(barrier, inc=1, device_id=dev, device_id_type=MESH)
    pl.semaphore_wait(barrier, 5)

    def remote(src, dst, send_sem, recv_sem, dev):
        return pltpu.make_async_remote_copy(
            src_ref=src, dst_ref=dst, send_sem=send_sem, recv_sem=recv_sem, device_id=dev, device_id_type=MESH
        )

    load_codes = pltpu.make_async_copy(codes_in, codes.at[z], load_sem.at[0])
    load_codes.start()
    load_kv = pltpu.make_async_copy(kvt.at[c], kv.at[0, :, pl.ds(c * tok, tok)], load_sem.at[1])
    load_kv.start()
    give_kv = remote(kvt.at[1 - c], kv.at[0, :, pl.ds(c * tok, tok)], pair_send.at[0], pair_recv.at[0], partner)
    give_kv.start()
    load_q = pltpu.make_async_copy(
        queries.at[:, pl.ds(pl.multiple_of(c * width, HD), width)], q.at[pl.ds(c * tok, tok)], load_sem.at[2]
    )
    load_q.start()
    give_q = remote(
        queries.at[:, pl.ds(pl.multiple_of((1 - c) * width, HD), width)],
        q.at[pl.ds(c * tok, tok)], pair_send.at[1], pair_recv.at[1], partner,
    )
    give_q.start()

    def part(block, a):
        return codes.at[block, pl.ds(pl.multiple_of(parity * half + a * quarter, quarter), quarter)]

    def share(block, a):
        dev = across_x + a * (across_y - across_x)
        ref = part(block, a)
        remote(ref, ref, xy_send.at[0], xy_recv.at[a * nz + block], (dev, s)).start()

    def zm_first(a):
        ref = part(z, a)
        remote(ref, ref, zm_send.at[0], zm_recv.at[a], down).start()

    def zp_first(a):
        ref = part(z, a)
        remote(ref, ref, zp_send.at[0], zp_recv.at[a], up).start()

    def zm_step(step, a):
        block = (z + step) % nz
        ref = part(block, a)
        remote(ref, ref, zm_send.at[0], zm_recv.at[(step - 1) * 2 + a], down).wait_recv()

        @pl.when(step < down_steps)
        def _():
            remote(ref, ref, zm_send.at[0], zm_recv.at[step * 2 + a], down).start()

        share(block, a)

    def zp_step(step, a):
        block = (z + nz - step) % nz
        ref = part(block, a)
        remote(ref, ref, zp_send.at[0], zp_recv.at[(step - 1) * 2 + a], up).wait_recv()

        @pl.when(step < up_steps)
        def _():
            remote(ref, ref, zp_send.at[0], zp_recv.at[step * 2 + a], up).start()

        share(block, a)

    def half_step(e):
        step, a = e // 2 + 1, e % 2

        @pl.when(step + down_steps_a <= down_steps)
        def _():
            zm_step(step + down_steps_a, a)

        @pl.when(step <= up_steps)
        def _():
            zp_step(step, a)

    load_codes.wait()
    zm_first(0)
    zm_first(1)
    load_kv.wait()
    mine = kv.at[0, :, pl.ds((1 - c) * tok, tok)]
    remote(mine, mine, pair_send.at[0], pair_recv.at[0], partner).wait_recv()

    def kv_send_from(t, part_index):
        ref = kv.at[t, part_index]
        remote(ref, kv.at[t + 1, part_index], kv_send.at[0], kv_recv.at[t * 4 + part_index], up).start()

    for part_index in range(4):
        kv_send_from(0, part_index)
    load_q.wait()
    mine = q.at[pl.ds((1 - c) * tok, tok)]
    remote(mine, mine, pair_send.at[1], pair_recv.at[1], partner).wait_recv()

    factor = math.log2(math.e) / math.sqrt(HD)

    def attend(t, head, group, mode):
        q_rows = q[:, pl.ds(pl.multiple_of(head * HD, HD), HD)]
        scores = lax.dot_general(
            q_rows, kv[t, 2 * group], (((1,), (1,)), ((), ())), preferred_element_type=F32
        )
        if mode != "full":
            i = lax.broadcasted_iota(jnp.int32, (rows, rows), 0)
            j = lax.broadcasted_iota(jnp.int32, (rows, rows), 1)
            scores = jnp.where(j <= i if mode == "own" else j > i, scores, -1e30)
        row_max = jnp.max(scores, axis=1, keepdims=True)
        if mode == "own":
            new_top = jnp.broadcast_to(row_max, (rows, HD))
        else:
            old_top = top[head]
            new_top = jnp.maximum(old_top, row_max)
        top[head] = new_top
        spread = jnp.concatenate([new_top] * (rows // HD), axis=1)
        weights = jnp.exp2((scores - spread) * factor).astype(BF16)
        values = jnp.concatenate([kv[t, 2 * group + 1], jnp.ones((rows, HD), BF16)], axis=1)
        product = jnp.dot(weights, values, preferred_element_type=F32)
        if mode != "own":
            fade = jnp.exp2((old_top - new_top) * factor)
            product = product + acc[head] * jnp.concatenate([fade, fade], axis=1)
        acc[head] = product

    quad = half_heads // 4

    def attend_quad(t, index, mode):
        def two(i, carry):
            head = index * quad + 2 * i
            attend(t, head, index // 2, mode)
            attend(t, head + 1, index // 2, mode)
            return carry

        lax.fori_loop(0, quad // 2, two, 0)

    def phase_a(t, carry):
        for index in range(4):
            ref = kv.at[t, index]
            remote(ref, ref, kv_send.at[0], kv_recv.at[(t - 1) * 4 + index], up).wait_recv()

            @pl.when(t < hops)
            def _():
                kv_send_from(t, index)

            if index < 3:
                e = (t - 1) * 3 + index
                zm_step(e // 2 + 1, e % 2)

            @pl.when(t == 1)
            def _():
                attend_quad(0, index, "own")

            @pl.when((t > 1) & (z >= t - 1))
            def _():
                attend_quad(t - 1, index, "full")

        return carry

    lax.fori_loop(1, hops + 1, phase_a, 0)
    zp_first(0)
    zp_first(1)
    for index in range(4):
        half_step(jnp.int32(index))

        @pl.when(z >= hops)
        def _():
            attend_quad(hops, index, "far")

    matrix = had[...]
    stacked = jnp.concatenate([matrix, matrix], axis=0)

    def rotate(head):
        both = acc[head]
        value = both[:, :HD] / both[:, HD:] * signs[c * half_heads + head]
        first = value.astype(BF16)
        rest = value - first.astype(F32)
        second = rest.astype(BF16)
        third = (rest - second.astype(F32)).astype(BF16)
        mixed = jnp.dot(jnp.concatenate([first, second], axis=1), stacked, preferred_element_type=F32)
        mixed = mixed + jnp.dot(third, matrix, preferred_element_type=F32)
        column = pl.multiple_of((c * half_heads + head) * HD, HD)
        xr[:, pl.ds(column, HD)] = (mixed * (1.0 / math.sqrt(HD))).astype(BF16)

    def rotate_two(i, carry):
        rotate(2 * i)
        rotate(2 * i + 1)
        return carry

    lax.fori_loop(0, half_heads // 4, rotate_two, 0)
    half_step(jnp.int32(4))
    lax.fori_loop(half_heads // 4, half_heads // 2, rotate_two, 0)
    half_step(jnp.int32(5))
    my_columns = xr.at[:, pl.ds(pl.multiple_of(c * width, HD), width)]
    swap = remote(my_columns, my_columns, xr_send.at[0], xr_recv.at[0], partner)
    swap.start()

    pairs = nz // 2
    first_pairs = down_steps_a // 2

    def origins(u):
        late = (u // first_pairs + 1) // 2
        k = u - first_pairs
        one = (1 - late) * 2 * u + late * (down_steps_a + k)
        two = (1 - late) * (2 * u + 1) + late * (nz - 1 - k)
        return (z + one) % nz, (z + two) % nz

    def unpack(block, side):
        column = pl.multiple_of((block * CORES + c) * HD, HD)
        sc[...] = scales[:, pl.ds(column, HD)].astype(F32)

        def eight_heads(i, carry):
            scale_rows = sc[pl.ds(pl.multiple_of(i * 8, 8), 8), :]
            for n in range(8):
                start = pl.multiple_of(i * HD + n * (HD // 8), HD // 8)
                packed = codes[block, pl.ds(start, HD // 8), :] ^ jnp.int32(-2004318072)
                scale = jnp.broadcast_to(scale_rows[n : n + 1, :], (HD // 8, HD))
                for k in range(8):
                    shifted = packed << (28 - 4 * k) if k < 7 else packed
                    value = (shifted >> 28).astype(F32)
                    at = pl.multiple_of((i * 8 + n) * HD + k * (HD // 8), HD // 8)
                    wbuf[pl.ds(at, HD // 8), side * HD : (side + 1) * HD] = (value * scale).astype(BF16)
            return carry

        lax.fori_loop(0, HEADS // 8, eight_heads, 0)

    def send_out(u):
        for side, block in enumerate(origins(u)):
            columns = pl.ds(pl.multiple_of((block * CORES + c) * HD, HD), HD)
            pltpu.make_async_copy(
                obuf.at[u, side, pl.ds(c * tok, tok)], out.at[:, columns], out_local.at[0]
            ).start()
            remote(
                obuf.at[u, side, pl.ds((1 - c) * tok, tok)], out.at[:, columns], out_send.at[0], out_recv.at[0], partner
            ).start()

    def shared(block):
        for a in range(2):
            ref = codes.at[block, pl.ds(pl.multiple_of((1 - parity) * half + a * quarter, quarter), quarter)]
            dev = across_x if a == 0 else across_y
            remote(ref, ref, xy_send.at[0], xy_recv.at[a * nz + block], (dev, s)).wait_recv()

    def project(u, carry):
        half_step(u + 6)

        @pl.when(u == 0)
        def _():
            theirs = xr.at[:, pl.ds(pl.multiple_of((1 - c) * width, HD), width)]
            remote(theirs, theirs, xr_send.at[0], xr_recv.at[0], partner).wait_recv()

        one, two = origins(u)

        @pl.when(u > 0)
        def _():
            shared(one)

        shared(two)
        unpack(one, 0)
        unpack(two, 1)
        total = jnp.dot(xr[...], wbuf[...], preferred_element_type=F32).astype(BF16)
        obuf[u, 0] = total[:, :HD]
        obuf[u, 1] = total[:, HD:]

        @pl.when(u > 0)
        def _():
            send_out(u - 1)

        return carry

    lax.fori_loop(0, pairs, project, 0)

    sent = codes.at[pl.ds(0, down_steps), pl.ds(0, half)]
    remote(sent, sent, zm_send.at[0], zm_recv.at[0], down).wait_send()
    sent = codes.at[pl.ds(0, up_steps), pl.ds(0, half)]
    remote(sent, sent, zp_send.at[0], zp_recv.at[0], up).wait_send()
    sent = codes.at[pl.ds(0, nz - 1), pl.ds(0, half)]
    remote(sent, sent, xy_send.at[0], xy_recv.at[0], (across_x, s)).wait_send()
    sent = kv.at[pl.ds(0, hops)]
    remote(sent, sent, kv_send.at[0], kv_recv.at[0], up).wait_send()
    give_kv.wait_send()
    give_q.wait_send()
    swap.wait_send()
    send_out(pairs - 1)
    moved = obuf.at[:, :, pl.ds(0, tok)]
    pltpu.make_async_copy(moved, moved, out_local.at[0]).wait()
    whole = remote(moved, moved, out_send.at[0], out_recv.at[0], partner)
    whole.wait_send()
    whole.wait_recv()


def on_device(plane_y, queries, keys_values, head_signs, out_codes, out_scales):
    tok = queries.shape[0]
    ns = lax.axis_size("seq")
    nz = ns // CORES
    rows = tok * CORES
    hops = WINDOW // rows
    words, cols = out_codes.shape
    half_heads = HEADS // CORES
    down_steps_a = 3 * hops // 2
    up_steps = (nz - 1 - down_steps_a) // 2 + 1
    down_steps = nz - 1 - up_steps
    kvt = keys_values.reshape(tok, 2, CORES, KV // CORES, HD)
    kvt = jnp.transpose(kvt, (2, 3, 1, 0, 4)).reshape(CORES, KV, tok, HD)
    signs = head_signs.astype(F32).reshape(HEADS, 1, HD)
    had = jnp.asarray(hadamard_columns(), BF16)
    hbm = pl.BlockSpec(memory_space=pltpu.HBM)
    vmem = pl.BlockSpec(memory_space=pltpu.VMEM)
    dma = pltpu.SemaphoreType.DMA
    return pl.pallas_call(
        functools.partial(kernel, plane_y),
        out_shape=jax.ShapeDtypeStruct((tok, ns * cols), BF16),
        in_specs=[hbm, hbm, hbm, vmem, vmem, vmem],
        out_specs=hbm,
        scratch_shapes=[
            pltpu.VMEM((nz, words, cols), jnp.int32),
            pltpu.VMEM((hops + 1, KV, rows, HD), BF16),
            pltpu.VMEM((rows, half_heads * HD), BF16),
            pltpu.VMEM((half_heads, rows, 2 * HD), F32),
            pltpu.VMEM((half_heads, rows, HD), F32),
            pltpu.VMEM((rows, HEADS * HD), BF16),
            pltpu.VMEM((HEADS * HD, 2 * cols), BF16),
            pltpu.VMEM((nz // 2, 2, rows, cols), BF16),
            pltpu.VMEM((HEADS, HD), F32),
            dma((2 * down_steps,)),
            dma((2 * up_steps,)),
            dma((4 * hops,)),
            dma((2 * nz,)),
            dma((1,)),
            dma((1,)),
            dma((1,)),
            dma((1,)),
            dma((3,)),
            dma((2,)),
            dma((2,)),
            dma((1,)),
            dma((1,)),
            dma((1,)),
            dma((1,)),
            dma((1,)),
        ],
        compiler_params=pltpu.CompilerParams(
            collective_id=0, has_side_effects=True, vmem_limit_bytes=60 * 1024 * 1024
        ),
    )(queries, kvt, out_codes, out_scales, signs, had)


def solution(mesh):
    groups = mesh.shape["groups"]
    plane_y = 1 << (groups.bit_length() // 2)
    return jax.shard_map(
        functools.partial(on_device, plane_y),
        mesh=mesh,
        in_specs=(
            P(("groups", "seq"), None),
            P(("groups", "seq"), None, None),
            P(),
            P(None, "seq"),
            P(),
        ),
        out_specs=P(("groups", "seq"), None),
        check_vma=False,
    )
```

time: 380 us -> 132 us (0.35)
  the two profiles are of different devices: /device:TPU:1316 before, /device:TPU:37 now
where the time goes in v1:
time: 132 us
  Pallas kernels  126 us (95%)
  local copies, waits for them, and re-layouts  4.95 us (4%)
    pallas_call x1, Pallas kernels, on_device(): pl.pallas_call(functools.partial(kernel, plane_y), out_shape=jax.ShapeDty...  126 us
    unnamed x1, local copies, waits for them, and re-layouts  3.1 us

profile of v1, /device:TPU:37, one launch (start us, length us, event | category | flops | bytes accessed | tf_op | source)
XLA Modules:
  0.0 132.1 jit_solution(1949523881825196983)
XLA Ops:
  0.0 1.3 convert_element_type.3
  1.3 1.1 reshape.9
  2.4 0.7 copy.7
  3.2 125.8 %shard_map.64 = bf16[128,8192]{1,0:T(8,128)(2,1)} custom-call(bf16[128,4096]{1,0:T(8,128)(2,1)} %queries.1, bf16[2,4,128,128]{3,2,1,0:T(8,128)(2,1)} %bitcast.4, s32[512,128]{1,0:T(8,128)} %codes_in.1, bf16[32,8192]{1,0:T(8,128)(2,1)} %scales.1, f32[32,1,128]{2,1,0:T(1,128)} %bitcast.5, bf16[128,128]{1,0:T(8,128)(2,1)} %constant.2.clone.had), custom_call_target="tpu_custom_call" | custom-call | tf_op jit(solution)/shard_map/pallas_call | solution.py:367
  129.0 3.1 %copy.9 = bf16[128,8192]{1,0:T(8,128)(2,1)} copy(bf16[128,8192]{1,0:T(8,128)(2,1)} %shard_map.64) | data formatting | bytes 4194304

commit v2 on v1

v2 whole, which is shorter than its diff:
```python
import functools
import math

import jax
import jax.numpy as jnp
import numpy as np
from jax import lax
from jax.experimental import pallas as pl
from jax.experimental.pallas import tpu as pltpu
from jax.sharding import PartitionSpec as P

HEADS = 32
KV = 4
HD = 128
WINDOW = 2048
CORES = 2
MESH = pl.DeviceIdType.MESH
F32 = jnp.float32
BF16 = jnp.bfloat16


def hadamard_columns():
    d = np.arange(HD)
    e = np.array([8 * i + k for k in range(8) for i in range(HD // 8)])
    common = d[:, None] & e[None, :]
    bits = sum((common >> b) & 1 for b in range(HD.bit_length()))
    return np.where(bits % 2 == 0, 1.0, -1.0).astype(np.float32)


def kernel(
    plane_y,
    queries, kv_in, codes_in, scales, signs, had,
    out,
    codes, kv, q, acc, top, xr, weights_even, weights_odd, partial, obuf,
    zm_recv, zp_recv, kv_recv, xy_recv,
    zm_send, zp_send, kv_send, xy_send,
    load_sem, pair_send, pair_recv, xr_send, xr_recv, out_local, out_send, out_recv,
):
    ns = lax.axis_size("seq")
    nz = ns // CORES
    g = lax.axis_index("groups")
    s = lax.axis_index("seq")
    z = s // CORES
    c = s % CORES
    tok = queries.shape[0]
    rows = tok * CORES
    half_heads = HEADS // CORES
    width = half_heads * HD
    hops = WINDOW // rows
    words = codes_in.shape[0]
    half, quarter, eighth = words // 2, words // 4, words // 8

    gx_, gy_ = g // plane_y, g % plane_y
    across_x = (gx_ + 1 - 2 * (gx_ % 2)) * plane_y + gy_
    across_y = gx_ * plane_y + gy_ + 1 - 2 * (gy_ % 2)
    parity = (gx_ + gy_) % 2
    partner = (g, z * CORES + 1 - c)
    up = (g, (s + CORES) % ns)
    down = (g, (s + ns - CORES) % ns)

    down_steps_a, up_steps, down_steps = plan(nz, hops)

    barrier = pltpu.get_barrier_semaphore()
    for dev in (partner, up, down, (across_x, s), (across_y, s)):
        pl.semaphore_signal(barrier, inc=1, device_id=dev, device_id_type=MESH)
    pl.semaphore_wait(barrier, 5)

    def remote(src, dst, send_sem, recv_sem, dev):
        return pltpu.make_async_remote_copy(
            src_ref=src, dst_ref=dst, send_sem=send_sem, recv_sem=recv_sem, device_id=dev, device_id_type=MESH
        )

    load_codes = pltpu.make_async_copy(codes_in, codes.at[z], load_sem.at[0])
    load_codes.start()
    loads, gives = [], []
    for part_index in range(KV):
        for core, into in ((c, loads), (1 - c, gives)):
            column = (part_index % 2) * KV * HD + (core * (KV // CORES) + part_index // 2) * HD
            source = kv_in.at[:, pl.ds(pl.multiple_of(column, HD), HD)]
            target = kv.at[0, part_index, pl.ds(c * tok, tok)]
            if into is loads:
                copy = pltpu.make_async_copy(source, target, load_sem.at[2 + part_index])
            else:
                copy = remote(source, target, pair_send.at[1 + part_index], pair_recv.at[1 + part_index], partner)
            copy.start()
            into.append(copy)
    load_q = pltpu.make_async_copy(
        queries.at[:, pl.ds(pl.multiple_of(c * width, HD), width)], q.at[pl.ds(c * tok, tok)], load_sem.at[1]
    )
    load_q.start()
    give_q = remote(
        queries.at[:, pl.ds(pl.multiple_of((1 - c) * width, HD), width)],
        q.at[pl.ds(c * tok, tok)], pair_send.at[0], pair_recv.at[0], partner,
    )
    give_q.start()

    def piece(block, a):
        return codes.at[block, pl.ds(pl.multiple_of(parity * half + a * eighth, eighth), eighth)]

    def share(block, a):
        ref = codes.at[block, pl.ds(pl.multiple_of(parity * half + a * quarter, quarter), quarter)]
        dev = across_x + a * (across_y - across_x)
        remote(ref, ref, xy_send.at[0], xy_recv.at[a * nz + block], (dev, s)).start()

    def zm_first(a):
        ref = piece(z, a)
        remote(ref, ref, zm_send.at[0], zm_recv.at[a], down).start()

    def zp_first(a):
        ref = piece(z, a)
        remote(ref, ref, zp_send.at[0], zp_recv.at[a], up).start()

    def zm_step(step, a):
        block = (z + step) % nz
        ref = piece(block, a)
        remote(ref, ref, zm_send.at[0], zm_recv.at[(step - 1) * 4 + a], down).wait_recv()

        @pl.when(step < down_steps)
        def _():
            remote(ref, ref, zm_send.at[0], zm_recv.at[step * 4 + a], down).start()

        @pl.when(a % 2 == 1)
        def _():
            share(block, a // 2)

    def zp_step(step, a):
        block = (z + nz - step) % nz
        ref = piece(block, a)
        remote(ref, ref, zp_send.at[0], zp_recv.at[(step - 1) * 4 + a], up).wait_recv()

        @pl.when(step < up_steps)
        def _():
            remote(ref, ref, zp_send.at[0], zp_recv.at[step * 4 + a], up).start()

        @pl.when(a % 2 == 1)
        def _():
            share(block, a // 2)

    def both_ways(e):
        step, a = e // 4 + 1, e % 4

        @pl.when(step + down_steps_a <= down_steps)
        def _():
            zm_step(step + down_steps_a, a)

        @pl.when(step <= up_steps)
        def _():
            zp_step(step, a)

    load_codes.wait()
    for a in range(4):
        zm_first(a)

    def kv_copy(t, part_index):
        at = t * 4 + part_index
        return remote(kv.at[t, part_index], kv.at[t + 1, part_index], kv_send.at[at], kv_recv.at[at], up)

    def kv_send_from(t, part_index):
        @pl.when((z >= t) & (z < nz - 1))
        def _():
            kv_copy(t, part_index).start()

    for part_index in range(4):
        loads[part_index].wait()
        mine = kv.at[0, part_index, pl.ds((1 - c) * tok, tok)]
        remote(mine, mine, pair_send.at[1 + part_index], pair_recv.at[1 + part_index], partner).wait_recv()
        kv_send_from(0, part_index)
    load_q.wait()
    mine = q.at[pl.ds((1 - c) * tok, tok)]
    remote(mine, mine, pair_send.at[0], pair_recv.at[0], partner).wait_recv()

    factor = math.log2(math.e) / math.sqrt(HD)

    def attend(t, head, group, mode):
        q_rows = q[:, pl.ds(pl.multiple_of(head * HD, HD), HD)]
        scores = lax.dot_general(
            q_rows, kv[t, 2 * group], (((1,), (1,)), ((), ())), preferred_element_type=F32
        )
        if mode != "full":
            i = lax.broadcasted_iota(jnp.int32, (rows, rows), 0)
            j = lax.broadcasted_iota(jnp.int32, (rows, rows), 1)
            scores = jnp.where(j <= i if mode == "own" else j > i, scores, -1e30)
        row_max = jnp.max(scores, axis=1, keepdims=True)
        if mode == "own":
            new_top = jnp.broadcast_to(row_max, (rows, HD))
        else:
            old_top = top[head]
            new_top = jnp.maximum(old_top, row_max)
        top[head] = new_top
        spread = jnp.concatenate([new_top] * (rows // HD), axis=1)
        weights = jnp.exp2((scores - spread) * factor).astype(BF16)
        values = jnp.concatenate([kv[t, 2 * group + 1], jnp.ones((rows, HD), BF16)], axis=1)
        product = jnp.dot(weights, values, preferred_element_type=F32)
        if mode != "own":
            fade = jnp.exp2((old_top - new_top) * factor)
            product = product + acc[head] * jnp.concatenate([fade, fade], axis=1)
        acc[head] = product

    quad = half_heads // 4

    def attend_two(t, index, i, mode):
        head = index * quad + 2 * i
        attend(t, head, index // 2, mode)
        attend(t, head + 1, index // 2, mode)

    def phase_a(t, carry):
        @pl.when(t == hops)
        def _():
            for a in range(4):
                zp_first(a)

        for index in range(4):
            @pl.when(z >= t)
            def _():
                ref = kv.at[t, index]
                remote(ref, ref, kv_send.at[0], kv_recv.at[(t - 1) * 4 + index], up).wait_recv()

            @pl.when(t < hops)
            def _():
                kv_send_from(t, index)

            for i in range(2):
                if index * 2 + i < 7:
                    e = (t - 1) * 7 + index * 2 + i
                    zm_step(e // 4 + 1, e % 4)

                @pl.when(t == 1)
                def _():
                    attend_two(0, index, i, "own")

                @pl.when((t > 1) & (z >= t - 1))
                def _():
                    attend_two(t - 1, index, i, "full")

        return carry

    lax.fori_loop(1, hops + 1, phase_a, 0)

    matrix = had[...]
    stacked = jnp.concatenate([matrix, matrix], axis=0)

    def rotate(head):
        both = acc[head]
        value = both[:, :HD] / both[:, HD:] * signs[pl.ds(c * half_heads + head, 1), :].astype(F32)
        first = value.astype(BF16)
        rest = value - first.astype(F32)
        second = rest.astype(BF16)
        third = (rest - second.astype(F32)).astype(BF16)
        mixed = jnp.dot(jnp.concatenate([first, second], axis=1), stacked, preferred_element_type=F32)
        mixed = mixed + jnp.dot(third, matrix, preferred_element_type=F32)
        column = pl.multiple_of((c * half_heads + head) * HD, HD)
        xr[:, pl.ds(column, HD)] = (mixed * (1.0 / math.sqrt(HD))).astype(BF16)

    def rotate_two(i, carry):
        rotate(2 * i)
        rotate(2 * i + 1)
        return carry

    swap_width = quad * HD

    def swapped(core, index):
        columns = xr.at[:, pl.ds(pl.multiple_of(core * width + index * swap_width, swap_width), swap_width)]
        return remote(columns, columns, xr_send.at[index], xr_recv.at[index], partner)

    def last_quad(index, carry):
        both_ways(2 * index)

        @pl.when(z >= hops)
        def _():
            attend_two(hops, index, 0, "far")
            attend_two(hops, index, 1, "far")

        both_ways(2 * index + 1)

        @pl.when(index > 0)
        def _():
            swapped(c, index - 1).start()

        rotate_two(2 * index, 0)
        rotate_two(2 * index + 1, 0)
        return carry

    lax.fori_loop(0, 4, last_quad, 0)
    both_ways(jnp.int32(8))
    swapped(c, 3).start()
    both_ways(jnp.int32(9))

    pairs = nz // 2
    first_pairs = down_steps_a // 2

    def origins(u):
        late = (u // first_pairs + 1) // 2
        k = u - first_pairs
        one = (1 - late) * 2 * u + late * (down_steps_a + k)
        two = (1 - late) * (2 * u + 1) + late * (nz - 1 - k)
        return (z + one) % nz, (z + two) % nz

    def scale_rows(block):
        column = pl.multiple_of((block * CORES + c) * HD, HD)
        return scales[:, pl.ds(column, HD)].astype(F32)

    def unpack(block, side, weights, rows_of_scales, heads):
        for n in heads:
            packed = codes[block, n * (HD // 8) : (n + 1) * (HD // 8), :] ^ jnp.int32(-2004318072)
            scale = jnp.broadcast_to(rows_of_scales[n : n + 1, :], (HD // 8, HD)).astype(BF16)
            for k in range(8):
                shifted = packed << (28 - 4 * k) if k < 7 else packed
                value = (shifted >> 28).astype(F32).astype(BF16)
                at = n * HD + k * (HD // 8)
                weights[at : at + HD // 8, side * HD : (side + 1) * HD] = value * scale

    def send_out(u):
        for side, block in enumerate(origins(u)):
            columns = pl.ds(pl.multiple_of((block * CORES + c) * HD, HD), HD)
            pltpu.make_async_copy(
                obuf.at[u, side, pl.ds(c * tok, tok)], out.at[:, columns], out_local.at[0]
            ).start()
            remote(
                obuf.at[u, side, pl.ds((1 - c) * tok, tok)], out.at[:, columns], out_send.at[0], out_recv.at[0], partner
            ).start()

    def shared(block):
        for a in range(2):
            ref = codes.at[block, pl.ds(pl.multiple_of((1 - parity) * half + a * quarter, quarter), quarter)]
            dev = across_x if a == 0 else across_y
            remote(ref, ref, xy_send.at[0], xy_recv.at[a * nz + block], (dev, s)).wait_recv()

    def arrived(u):
        one, two = origins(u)

        @pl.when(u > 0)
        def _():
            shared(one)

        shared(two)

    depth = 2 * HD

    def project(u, weights, later):
        both_ways(10 + 2 * u)

        @pl.when(u < pairs - 1)
        def _():
            arrived(u + 1)

        both = origins((u + 1) % pairs)

        def beside(steps, total):
            scale_both = [scale_rows(block) for block in both]
            for n in steps:
                for side in range(2):
                    unpack(both[side], side, later, scale_both[side], (2 * n, 2 * n + 1))
                columns = slice(n * depth, (n + 1) * depth)
                product = jnp.dot(xr[:, columns], weights[columns, :], preferred_element_type=F32)
                total = product if total is None else total + product
            return total

        steps = HEADS // 2
        partial[...] = beside(range(steps // 2), None)
        both_ways(11 + 2 * u)
        total = partial[...] + beside(range(steps // 2, steps), None)
        total = total.astype(BF16)
        obuf[u, 0] = total[:, :HD]
        obuf[u, 1] = total[:, HD:]

        @pl.when(u > 0)
        def _():
            send_out(u - 1)

    def two_pairs(v, carry):
        project(2 * v, weights_even, weights_odd)
        project(2 * v + 1, weights_odd, weights_even)
        return carry

    arrived(jnp.int32(0))
    one, two = origins(jnp.int32(0))
    unpack(one, 0, weights_even, scale_rows(one), range(HEADS))
    unpack(two, 1, weights_even, scale_rows(two), range(HEADS))
    for index in range(4):
        swapped(1 - c, index).wait_recv()
    lax.fori_loop(0, pairs // 2, two_pairs, 0)

    sent = codes.at[pl.ds(0, down_steps), pl.ds(0, half)]
    remote(sent, sent, zm_send.at[0], zm_recv.at[0], down).wait_send()
    sent = codes.at[pl.ds(0, up_steps), pl.ds(0, half)]
    remote(sent, sent, zp_send.at[0], zp_recv.at[0], up).wait_send()
    sent = codes.at[pl.ds(0, nz - 1), pl.ds(0, half)]
    remote(sent, sent, xy_send.at[0], xy_recv.at[0], (across_x, s)).wait_send()

    def kv_left(t, carry):
        @pl.when((z >= t) & (z < nz - 1))
        def _():
            for part_index in range(4):
                kv_copy(t, part_index).wait_send()

        return carry

    lax.fori_loop(0, hops, kv_left, 0)
    give_q.wait_send()
    for index in range(4):
        gives[index].wait_send()
        swapped(c, index).wait_send()
    send_out(pairs - 1)
    moved = obuf.at[:, :, pl.ds(0, tok)]
    pltpu.make_async_copy(moved, moved, out_local.at[0]).wait()
    whole = remote(moved, moved, out_send.at[0], out_recv.at[0], partner)
    whole.wait_send()
    whole.wait_recv()


def plan(nz, hops):
    down_beside = 7 * hops // 4
    up_steps = (nz - 1 - down_beside) // 2 + 1
    return down_beside, up_steps, nz - 1 - up_steps


def on_device(plane_y, queries, keys_values, head_signs, out_codes, out_scales):
    tok = queries.shape[0]
    ns = lax.axis_size("seq")
    nz = ns // CORES
    rows = tok * CORES
    hops = WINDOW // rows
    words, cols = out_codes.shape
    half_heads = HEADS // CORES
    _, up_steps, down_steps = plan(nz, hops)
    kv_rows = keys_values.reshape(tok, 2 * KV * HD)
    had = jnp.asarray(hadamard_columns(), BF16)
    hbm = pl.BlockSpec(memory_space=pltpu.HBM)
    vmem = pl.BlockSpec(memory_space=pltpu.VMEM)
    dma = pltpu.SemaphoreType.DMA
    return pl.pallas_call(
        functools.partial(kernel, plane_y),
        out_shape=jax.ShapeDtypeStruct((tok, ns * cols), BF16),
        in_specs=[hbm, hbm, hbm, vmem, vmem, vmem],
        out_specs=hbm,
        scratch_shapes=[
            pltpu.VMEM((nz, words, cols), jnp.int32),
            pltpu.VMEM((hops + 1, KV, rows, HD), BF16),
            pltpu.VMEM((rows, half_heads * HD), BF16),
            pltpu.VMEM((half_heads, rows, 2 * HD), F32),
            pltpu.VMEM((half_heads, rows, HD), F32),
            pltpu.VMEM((rows, HEADS * HD), BF16),
            pltpu.VMEM((HEADS * HD, 2 * cols), BF16),
            pltpu.VMEM((HEADS * HD, 2 * cols), BF16),
            pltpu.VMEM((rows, 2 * cols), F32),
            pltpu.VMEM((nz // 2, 2, rows, cols), BF16),
            dma((4 * down_steps,)),
            dma((4 * up_steps,)),
            dma((4 * hops,)),
            dma((2 * nz,)),
            dma((1,)),
            dma((1,)),
            dma((4 * hops,)),
            dma((1,)),
            dma((2 + KV,)),
            dma((1 + KV,)),
            dma((1 + KV,)),
            dma((4,)),
            dma((4,)),
            dma((1,)),
            dma((1,)),
            dma((1,)),
        ],
        compiler_params=pltpu.CompilerParams(
            collective_id=0, has_side_effects=True, vmem_limit_bytes=60 * 1024 * 1024
        ),
    )(queries, kv_rows, out_codes, out_scales, head_signs, had)


def solution(mesh):
    groups = mesh.shape["groups"]
    plane_y = 1 << (groups.bit_length() // 2)
    return jax.shard_map(
        functools.partial(on_device, plane_y),
        mesh=mesh,
        in_specs=(
            P(("groups", "seq"), None),
            P(("groups", "seq"), None, None),
            P(),
            P(None, "seq"),
            P(),
        ),
        out_specs=P(("groups", "seq"), None),
        check_vma=False,
    )
```

time: 132 us -> 123 us (0.932)
  Pallas kernels: 126 us -> 118 us
    pallas_call x1, Pallas kernels: 126 us -> 118 us  [on_device(): pl.pallas_call(functools.partial(kernel, plane_y), out_shape=jax.ShapeDty...]
    reshape x2 -> x0, local copies, waits for them, and re-layouts: 1.86 us -> none  [on_device(): kvt = keys_values.reshape(tok, 2, CORES, KV // CORES, HD)]
    unnamed x1 -> x2, local copies, waits for them, and re-layouts: 3.1 us -> 4.78 us
where the time goes in v2:
time: 123 us
  Pallas kernels  118 us (96%)
  local copies, waits for them, and re-layouts  4.78 us (4%)
    pallas_call x1, Pallas kernels, on_device(): pl.pallas_call(functools.partial(kernel, plane_y), out_shape=jax.ShapeDty...  118 us
    unnamed x2, local copies, waits for them, and re-layouts  4.78 us

profile of v2, /device:TPU:37, one launch (start us, length us, event | category | flops | bytes accessed | tf_op | source)
XLA Modules:
  0.0 122.8 jit_solution(4505300986602354641)
XLA Ops:
  0.0 1.7 %copy.7 = bf16[16,8,2,512]{3,1,2,0:T(8,128)(2,1)} copy(bf16[16,8,2,512]{3,2,1,0:T(2,128)(2,1)} %bitcast.3) | data formatting | bytes 524288
  1.7 118.0 %shard_map.64 = bf16[128,8192]{1,0:T(8,128)(2,1)} custom-call(bf16[128,4096]{1,0:T(8,128)(2,1)} %queries.1, bf16[128,1024]{1,0:T(8,128)(2,1)} %bitcast.2, s32[512,128]{1,0:T(8,128)} %codes_in.1, bf16[32,8192]{1,0:T(8,128)(2,1)} %scales.1, s32[32,128]{1,0:T(8,128)} %signs.1, bf16[128,128]{1,0:T(8,128)(2,1)} %constant.2.clone.had), custom_call_target="tpu_custom_call" | custom-call | tf_op jit(solution)/shard_map/pallas_call | solution.py:431
  119.7 3.1 %copy.9 = bf16[128,8192]{1,0:T(8,128)(2,1)} copy(bf16[128,8192]{1,0:T(8,128)(2,1)} %shard_map.64) | data formatting | bytes 4194304

commit v3 on v2

--- a/solution.py
+++ b/solution.py
@@ -281,9 +281,7 @@
         return carry
 
     lax.fori_loop(0, 4, last_quad, 0)
-    both_ways(jnp.int32(8))
     swapped(c, 3).start()
-    both_ways(jnp.int32(9))
 
     pairs = nz // 2
     first_pairs = down_steps_a // 2
@@ -337,7 +335,7 @@
     depth = 2 * HD
 
     def project(u, weights, later):
-        both_ways(10 + 2 * u)
+        both_ways(8 + 2 * u)
 
         @pl.when(u < pairs - 1)
         def _():
@@ -357,7 +355,7 @@
 
         steps = HEADS // 2
         partial[...] = beside(range(steps // 2), None)
-        both_ways(11 + 2 * u)
+        both_ways(9 + 2 * u)
         total = partial[...] + beside(range(steps // 2, steps), None)
         total = total.astype(BF16)
         obuf[u, 0] = total[:, :HD]

time: 123 us -> 125 us (1.016)
  Pallas kernels: 118 us -> 120 us
    pallas_call x1, Pallas kernels: 118 us -> 120 us  [on_device(): pl.pallas_call(functools.partial(kernel, plane_y), out_shape=jax.ShapeDty...]
where the time goes in v3:
time: 125 us
  Pallas kernels  120 us (96%)
  local copies, waits for them, and re-layouts  4.78 us (4%)
    pallas_call x1, Pallas kernels, on_device(): pl.pallas_call(functools.partial(kernel, plane_y), out_shape=jax.ShapeDty...  120 us
    unnamed x2, local copies, waits for them, and re-layouts  4.78 us

profile of v3, /device:TPU:37, one launch (start us, length us, event | category | flops | bytes accessed | tf_op | source)
XLA Modules:
  0.0 125.1 jit_solution(13283412929220748035)
XLA Ops:
  0.0 1.7 %copy.7 = bf16[16,8,2,512]{3,1,2,0:T(8,128)(2,1)} copy(bf16[16,8,2,512]{3,2,1,0:T(2,128)(2,1)} %bitcast.3) | data formatting | bytes 524288
  1.7 120.3 %shard_map.64 = bf16[128,8192]{1,0:T(8,128)(2,1)} custom-call(bf16[128,4096]{1,0:T(8,128)(2,1)} %queries.1, bf16[128,1024]{1,0:T(8,128)(2,1)} %bitcast.2, s32[512,128]{1,0:T(8,128)} %codes_in.1, bf16[32,8192]{1,0:T(8,128)(2,1)} %scales.1, s32[32,128]{1,0:T(8,128)} %signs.1, bf16[128,128]{1,0:T(8,128)(2,1)} %constant.2.clone.had), custom_call_target="tpu_custom_call" | custom-call | tf_op jit(solution)/shard_map/pallas_call | solution.py:429
  122.0 3.1 %copy.9 = bf16[128,8192]{1,0:T(8,128)(2,1)} copy(bf16[128,8192]{1,0:T(8,128)(2,1)} %shard_map.64) | data formatting | bytes 4194304
